TPU v7x, 32 devices: a whole 2x2x4 slice. The times are simulated.
32 devices in a mesh: ty: 4 (over z), tx: 8 (over y, x, core).
Axes of the slice: x: 2, y: 2, z: 4, core: 2. Of those that a mesh axis runs over, the one named last changes fastest.
Arguments:
- object_slices: float32 [2, 2, 2048, 4096], P(None, None, 'ty', 'tx'), may hold values from -4 to 4
- probe_modes: float32 [4, 2, 128, 128], replicated, may hold values from -12 to 12
- patterns: bfloat16 [256, 128, 128], P(('ty', 'tx')), may hold values from 0 to 2
- positions: int32 [256, 2], replicated, may hold values from 0 to 4095, as said below
- counts: int32 [32], replicated, may hold values from 6 to 8, as said below
Outputs:
- new_object: float32 [2, 2, 2048, 4096], P(None, None, 'ty', 'tx')
- new_probe: float32 [4, 2, 128, 128], replicated
Inputs may be any that keep to these rules, and one draw needn't show every extreme that they name: positions[j] is the centre of pattern j, which was acquired by device j // 8 of ty+tx (ty slowest); its column lies in that device's column of tiles of 512 x 512 cells. Of the live patterns of one device, at most 2 lie in any one row of tiles; in every column of tiles some row of tiles holds exactly 2 live patterns from every device of that column. The live patterns of device d are its first counts[d] slots; some device has 8.
All inputs are finite; a program needn't handle non-finite values.
Results may differ from a plain program's by a relative error of at most 0.0085.
The roundings to bfloat16 on the way count: a program that leaves them out, or rounds other values in their place, can miss the bound.
Values may be sent and summed in bfloat16 or wider, within the bound.
No kernel may reach another device: no remote copies, remote signals or barrier semaphores. Data moves between devices by JAX's collectives and lax.ppermute only.
A program may use at most 128 MiB of HBM per device.

v0:
```python
import math
import jax
import jax.numpy as jnp
from jax import lax
from jax.sharding import PartitionSpec as P

CAP = 2
PROPAGATION = 0.37


def extended_2(block, sides, width):
    for axis, dim in sides:
        count = lax.axis_size(axis)
        forward = [(i, i + 1) for i in range(count - 1)]
        backward = [(target, source) for source, target in forward]
        low = lax.ppermute(
            lax.slice_in_dim(block, block.shape[dim] - width, None, axis=dim), axis, forward
        )
        high = lax.ppermute(lax.slice_in_dim(block, 0, width, axis=dim), axis, backward)
        block = jnp.concatenate([low, block, high], axis=dim)
    return block


def make_tables(extent):
    indices = jnp.arange(extent, dtype=jnp.int32)
    product = indices[:, None] * indices[None, :] % extent
    angles = 2.0 * jnp.pi / extent * product.astype(jnp.float32)
    norm_scale = 1.0 / math.sqrt(extent)
    real_table = (jnp.cos(angles) * norm_scale).astype(jnp.bfloat16)
    imag_table = (-jnp.sin(angles) * norm_scale).astype(jnp.bfloat16)
    right_fwd = jnp.concatenate(
        [
            jnp.concatenate([real_table, imag_table], 1),
            jnp.concatenate([-imag_table, real_table], 1),
        ],
        0,
    )
    right_inv = jnp.concatenate(
        [
            jnp.concatenate([real_table, -imag_table], 1),
            jnp.concatenate([imag_table, real_table], 1),
        ],
        0,
    )
    left_fwd = jnp.concatenate([real_table, imag_table], 0)
    left_inv = jnp.concatenate([real_table, -imag_table], 0)
    frequency = jnp.where(indices < extent // 2, indices, indices - extent).astype(jnp.float32)
    phases = -jnp.pi * PROPAGATION / extent * (frequency[:, None] ** 2 + frequency[None, :] ** 2)
    kernel = jnp.stack([jnp.cos(phases), jnp.sin(phases)])
    return (right_fwd, left_fwd, right_inv, left_inv, kernel)


def transform(wave_field, right_table, left_table):
    extent = wave_field.shape[-1]
    rounded = wave_field.astype(jnp.bfloat16)
    joined = jnp.concatenate([rounded[:, 0], rounded[:, 1]], axis=-1)
    partial_value = jnp.einsum(
        "bpk,kq->bpq", joined, right_table, preferred_element_type=jnp.float32
    ).astype(jnp.bfloat16)
    stacked = jnp.einsum(
        "ij,bjq->biq", left_table, partial_value, preferred_element_type=jnp.float32
    )
    real_part = stacked[:, :extent, :extent] - stacked[:, extent:, extent:]
    imag_part = stacked[:, extent:, :extent] + stacked[:, :extent, extent:]
    return jnp.stack([real_part, imag_part], axis=1)


def complex_product(former, latter):
    former_re = former[..., 0, :, :]
    former_im = former[..., 1, :, :]
    latter_re = latter[..., 0, :, :]
    latter_im = latter[..., 1, :, :]
    return jnp.stack(
        [
            former_re * latter_re - former_im * latter_im,
            former_re * latter_im + former_im * latter_re,
        ],
        axis=-3,
    )


def conjugate(values):
    return jnp.stack([values[..., 0, :, :], -values[..., 1, :, :]], axis=-3)


def pattern_terms(window, amplitude, live_flag, probe_modes, tables):
    right_fwd, left_fwd, right_inv, left_inv, kernel = tables
    slices = window.shape[0]
    inputs = [probe_modes]
    far_field = None
    for slice_index in range(slices):
        exit_wave = complex_product(inputs[slice_index], window[slice_index])
        if slice_index + 1 < slices:
            spread_wave = complex_product(kernel, transform(exit_wave, right_fwd, left_fwd))
            inputs.append(transform(spread_wave, right_inv, left_inv))
        else:
            far_field = transform(exit_wave, right_fwd, left_fwd)
    intensity = jnp.sum(far_field[:, 0] ** 2 + far_field[:, 1] ** 2, axis=0)
    factor = (1.0 - amplitude / jnp.sqrt(jnp.maximum(intensity, 0.25))) * live_flag
    residue = far_field * factor
    backward = transform(residue, right_inv, left_inv)
    slice_grads = [None] * slices
    for slice_index in reversed(range(slices)):
        slice_grads[slice_index] = jnp.sum(
            complex_product(conjugate(inputs[slice_index]), backward), axis=0
        )
        if slice_index > 0:
            inner_wave = transform(
                complex_product(conjugate(window[slice_index]), backward), right_fwd, left_fwd
            )
            backward = transform(
                complex_product(conjugate(kernel), inner_wave), right_inv, left_inv
            )
    probe_term = complex_product(conjugate(window[0]), backward)
    return (jnp.stack(slice_grads), probe_term)


def settle(centre, leading, trailing, axis, margin):
    length = centre.shape[axis]
    top_part = lax.slice_in_dim(centre, 0, margin, axis=axis) + leading
    middle_part = lax.slice_in_dim(centre, margin, length - margin, axis=axis)
    bottom_part = lax.slice_in_dim(centre, length - margin, length, axis=axis) + trailing
    return jnp.concatenate([top_part, middle_part, bottom_part], axis=axis)


def on_device(object_slices, probe_modes, patterns, positions, counts):
    slices = object_slices.shape[0]
    tile_cells = object_slices.shape[2]
    extent = probe_modes.shape[-1]
    margin = extent // 2
    per_device = patterns.shape[0]
    row_count = lax.axis_size("ty")
    column_count = lax.axis_size("tx")
    row_index = lax.axis_index("ty")
    column_index = lax.axis_index("tx")
    position_grid = positions.reshape(row_count, column_count, per_device, 2)
    column = lax.dynamic_index_in_dim(position_grid, column_index, axis=1, keepdims=False)
    count_grid = counts.reshape(row_count, column_count)
    column_counts = lax.dynamic_index_in_dim(count_grid, column_index, axis=1, keepdims=False)
    ordinal = jnp.arange(per_device, dtype=jnp.int32)
    is_live = ordinal[None, :] < column_counts[:, None]
    target = column[:, :, 0] // tile_cells
    earlier = ordinal[None, :] < ordinal[:, None]
    same_row = is_live[:, None, :] & (target[:, None, :] == target[:, :, None]) & earlier[None]
    row_rank = jnp.sum(same_row.astype(jnp.int32), axis=2)
    slot_count = row_count * CAP
    slot_ids = jnp.arange(slot_count, dtype=jnp.int32)
    own_live = lax.dynamic_index_in_dim(is_live, row_index, axis=0, keepdims=False)
    own_slot = lax.dynamic_index_in_dim(target * CAP + row_rank, row_index, axis=0, keepdims=False)
    choose = (own_live[None, :] & (own_slot[None, :] == slot_ids[:, None])).astype(jnp.bfloat16)
    outgoing = jnp.einsum(
        "sj,jab->sab", choose, patterns, preferred_element_type=jnp.float32
    ).astype(jnp.bfloat16)
    incoming = lax.all_to_all(outgoing, "ty", split_axis=0, concat_axis=0, tiled=True)
    rank_ids = jnp.arange(CAP, dtype=jnp.int32)
    matched = (
        is_live[:, None, :]
        & (target[:, None, :] == row_index)
        & (row_rank[:, None, :] == rank_ids[None, :, None])
    )
    slot_live = jnp.any(matched, axis=2).reshape(-1)
    chosen = matched.astype(jnp.int32)
    centre_row = jnp.sum(chosen * column[:, None, :, 0], axis=2).reshape(-1)
    centre_col = jnp.sum(chosen * column[:, None, :, 1], axis=2).reshape(-1)
    local_row = jnp.where(slot_live, centre_row - row_index * tile_cells, 0)
    local_col = jnp.where(slot_live, centre_col - column_index * tile_cells, 0)
    extended = extended_2(object_slices, (("ty", 2), ("tx", 3)), margin)
    tables = make_tables(extent)

    def visit_slot(running, element):
        gradient, probe_grad = running
        amplitude, row_start, col_start, live_flag = element
        corner = (jnp.int32(0), jnp.int32(0), row_start, col_start)
        window = lax.dynamic_slice(extended, corner, (slices, 2, extent, extent))
        slice_grads, probe_term = pattern_terms(
            window, amplitude.astype(jnp.float32), live_flag, probe_modes, tables
        )
        current = lax.dynamic_slice(gradient, corner, (slices, 2, extent, extent))
        gradient = lax.dynamic_update_slice(gradient, current + slice_grads, corner)
        return ((gradient, probe_grad + probe_term), None)

    span_cells = tile_cells + extent
    initial = (
        jnp.zeros((slices, 2, span_cells, span_cells), jnp.float32),
        jnp.zeros(probe_modes.shape, jnp.float32),
    )
    (gradient, probe_grad), unused = lax.scan(
        visit_slot, initial, (incoming, local_row, local_col, slot_live.astype(jnp.float32))
    )
    row_edges = jnp.concatenate([gradient[:, :, :margin], gradient[:, :, -margin:]], axis=2)
    row_halo = extended_2(row_edges, (("ty", 2),), margin)
    row_folded = settle(
        gradient[:, :, margin : margin + tile_cells],
        row_halo[:, :, :margin],
        row_halo[:, :, -margin:],
        2,
        margin,
    )
    col_edges = jnp.concatenate([row_folded[..., :margin], row_folded[..., -margin:]], axis=3)
    col_halo = extended_2(col_edges, (("tx", 3),), margin)
    folded = settle(
        row_folded[..., margin : margin + tile_cells],
        col_halo[..., :margin],
        col_halo[..., -margin:],
        3,
        margin,
    )
    probe_power = jnp.mean(jnp.sum(probe_modes**2, axis=(0, 1)))
    new_object = object_slices - folded / (probe_power + 1e-06)
    summed = lax.psum(probe_grad, ("ty", "tx"))
    spread = jnp.sqrt(jnp.mean(summed * summed) + 1e-06)
    new_probe = probe_modes - 0.5 * summed / spread
    return (new_object, new_probe)


def solution(mesh):
    return jax.shard_map(
        on_device,
        mesh=mesh,
        in_specs=(P(None, None, "ty", "tx"), P(), P(("ty", "tx"), None, None), P(), P()),
        out_specs=(P(None, None, "ty", "tx"), P()),
        check_vma=False,
    )
```

profile of v0, /device:TPU:0, one launch (start us, length us, event | category | flops | bytes accessed | tf_op | source)
XLA Modules:
  0.0 498.1 jit_solution(16212770416473145393)
XLA Ops:
  10.3 6.3 %all-to-all-start = ((bf16[8,128,128]{2,1,0:T(8,128)(2,1)}), bf16[8,128,128]{2,1,0:T(8,128)(2,1)}, u32[]{:S(2)}, u32[]{:S(2)}) async-start(bf16[8,128,128]{2,1,0:T(8,128)(2,1)} %copy.108), calls=%async_computation | async-start | bytes 524288 | tf_op jit(solution)/shard_map/all_to_all | solution.py:154
  18.0 4.0 collective-permute-start
  23.2 5.2 %copy.120 = f32[2,2,512,512]{2,3,1,0:T(8,128)} copy(f32[2,2,512,512]{3,2,1,0:T(8,128)} %param.7) | data formatting | bytes 8388608 | tf_op args[0]
  30.5 2.0 collective-permute-done
  32.8 4.0 collective-permute-done.1
  37.2 2.8 pad_maximum_fusion.4
  40.0 2.1 collective-permute-start.2
  47.4 5.9 %pad_maximum_fusion = f32[2,2,640,640]{2,3,1,0:T(8,128)} fusion(f32[2,2,640,64]{2,3,1,0:T(8,128)} %collective-permute-done.3, f32[2,2,64,512]{2,3,1,0:T(8,128)S(1)} %copy.106, f32[2,2,512,512]{2,3,1,0:T(8,128)} %copy.120, f32[2,2,64,512]{2,3,1,0:T(8,128)S(1)} %copy.104, f32[2,2,640,64]{2,3,1,0:T(8,128)} %collective-permute-done.2), kind=kLoop, calls=%fused_computation.110 | loop fusion | flops 6553600 | bytes 13107200 | tf_op jit(solution)/shard_map/concatenate | solution.py:20
  53.3 3.2 broadcast_in_dim.8
  56.5 217.4 %while.18 = (s32[]{:T(128)}, f32[2,2,640,640]{2,3,1,0:T(8,128)}, f32[4,2,128,128]{3,2,0,1:T(8,128)S(1)}, s32[8]{0:T(128)S(1)}, s32[8]{0:T(128)S(1)}, /*index=5*/...) while((s32[]{:T(128)}, f32[2,2,640,640]{2,3,1,0:T(8,128)}, ...), condition=%wide.region_8.9_spmd.clone.clone.clone.clone, body=%wide.region_4.8_spmd.clone.clone.clone.clone.sunk | while | flops 815677440 | bytes 33391468 | solution.py:187
  67.7 1.5 convolution_bitcast_fusion.13
  70.0 1.5 convolution_bitcast_fusion.14
  71.5 1.5 fusion.155
  73.7 1.5 convolution_bitcast_fusion.15
  79.3 4.4 dynamic_update_slice.10
  94.9 1.5 convolution_bitcast_fusion.13
  97.1 1.5 convolution_bitcast_fusion.14
  100.9 1.5 convolution_bitcast_fusion.15
  106.5 4.2 dynamic_update_slice.10
  121.9 1.5 convolution_bitcast_fusion.13
  124.2 1.5 convolution_bitcast_fusion.14
  127.9 1.5 convolution_bitcast_fusion.15
  133.5 4.4 dynamic_update_slice.10
  149.1 1.5 convolution_bitcast_fusion.13
  151.4 1.5 convolution_bitcast_fusion.14
  152.9 1.5 fusion.155
  155.1 1.5 convolution_bitcast_fusion.15
  160.7 4.4 dynamic_update_slice.10
  176.3 1.5 convolution_bitcast_fusion.13
  178.6 1.5 convolution_bitcast_fusion.14
  182.3 1.5 convolution_bitcast_fusion.15
  187.9 4.4 dynamic_update_slice.10
  203.5 1.5 convolution_bitcast_fusion.13
  205.7 1.5 convolution_bitcast_fusion.14
  209.5 1.5 convolution_bitcast_fusion.15
  215.1 4.3 dynamic_update_slice.10
  230.6 1.5 convolution_bitcast_fusion.13
  232.9 1.5 convolution_bitcast_fusion.14
  236.6 1.5 convolution_bitcast_fusion.15
  242.2 4.4 dynamic_update_slice.10
  257.8 1.5 convolution_bitcast_fusion.13
  260.1 1.5 convolution_bitcast_fusion.14
  263.9 1.5 convolution_bitcast_fusion.15
  269.4 4.4 dynamic_update_slice.10
  273.8 8.2 %copy.114 = f32[2,2,640,640]{3,2,1,0:T(8,128)} copy(f32[2,2,640,640]{2,3,1,0:T(8,128)} %get-tuple-element.206) | data formatting | bytes 13107200 | tf_op jit(solution)/shard_map/while | solution.py:187
  283.1 1.9 collective-permute-start.4
  285.0 8.0 %collective-permute-done.4 = f32[2,2,64,640]{3,2,1,0:T(8,128)S(1)} collective-permute-done((f32[2,2,64,640]{3,2,1,0:T(8,128)S(1)}, f32[2,2,64,640]{3,2,1,0:T(8,128)S(1)}, u32[]{:S(2)}, u32[]{:S(2)}) %collective-permute-start.4) | collective-permute-done | bytes 655392 | tf_op jit(solution)/shard_map/ppermute | solution.py:16
  293.1 2.3 slice_add_fusion.7
  295.3 1.5 collective-permute-start.5
  296.8 4.2 slice.281
  301.4 7.1 %collective-permute-done.5 = f32[2,2,64,640]{3,2,1,0:T(8,128)S(1)} collective-permute-done((f32[2,2,64,640]{3,2,1,0:T(8,128)}, f32[2,2,64,640]{3,2,1,0:T(8,128)S(1)}, u32[]{:S(2)}, u32[]{:S(2)}) %collective-permute-start.5) | collective-permute-done | bytes 655392 | tf_op jit(solution)/shard_map/ppermute | solution.py:19
  308.5 2.0 slice_add_fusion.6
  310.5 1.5 copy.119
  312.0 2.0 pad_maximum_fusion.6
  314.0 14.0 %collective-permute-start.6 = (f32[2,2,512,64]{2,3,1,0:T(8,128)}, f32[2,2,512,64]{2,3,1,0:T(8,128)}, u32[]{:S(2)}, u32[]{:S(2)}) collective-permute-start(f32[2,2,512,64]{2,3,1,0:T(8,128)} %pad_maximum_fusion.6), channel_id=1, source_target_pairs={{0,1},{1,2},{2,3},{3,4},{4,5},{5,6},{6,7},{8,9},{9,10},{10,11},{11... | collective-permute-start | bytes 1572872 | tf_op jit(solution)/shard_map/ppermute | solution.py:16
  329.1 2.7 maximum_add_fusion.3
  333.0 136.7 %all-reduce.2.cloned.1.call-done = f32[4,2,128,128]{3,2,1,0:T(8,128)} async-done(((f32[4,2,128,128]{3,2,1,0:T(8,128)}), f32[4,2,128,128]{3,2,1,0:T(8,128)}) %all-reduce.2.cloned.1.call-update) | async-done | bytes 524304 | tf_op jit(solution)/shard_map/psum | solution.py:210
  469.7 1.8 multiply_reduce_fusion
  472.2 2.5 divide_subtract_fusion
  475.4 3.9 pad_maximum_fusion.1
  479.6 1.8 copy-done.2
  481.4 1.7 maximum_add_fusion.2
  483.1 3.0 fusion.85
  486.1 5.2 %copy.122 = f32[2,2,512,512]{3,2,1,0:T(8,128)} copy(f32[2,2,512,512]{2,3,1,0:T(8,128)} %fusion.85) | data formatting | bytes 8388608
  (355 shorter events, 128.7 us)
Async XLA Ops:
  7.2 2.1 copy-start
  10.3 43.0 %all-to-all-start = ((bf16[8,128,128]{2,1,0:T(8,128)(2,1)}), bf16[8,128,128]{2,1,0:T(8,128)(2,1)}, u32[]{:S(2)}, u32[]{:S(2)}) async-start(bf16[8,128,128]{2,1,0:T(8,128)(2,1)} %copy.108), calls=%async_computation | async-start | bytes 524288 | tf_op jit(solution)/shard_map/all_to_all | solution.py:154
  16.7 453.1 %all-reduce.2.cloned.1.call-start = ((), (), s32[]{:S(2)}) async-start(), calls=%async_computation.1 | async-start | bytes 1048576 | tf_op jit(solution)/shard_map/psum | solution.py:210
  18.0 14.5 %collective-permute-start = (f32[2,2,64,512]{3,2,1,0:T(8,128)S(1)}, f32[2,2,64,512]{3,2,1,0:T(8,128)S(1)}, u32[]{:S(2)}, u32[]{:S(2)}) collective-permute-start(f32[2,2,64,512]{3,2,1,0:T(8,128)S(1)} %get-tuple-element.545), channel_id=1, source_target_pairs={{0,8},{8,16},{16,24},{1,9},{9,17},{17,25},{2,10},{10,18},{18,26},{... | collective-permute-start | bytes 1572872 | tf_op jit(solution)/shard_map/ppermute | solution.py:16
  21.9 14.9 %collective-permute-start.1 = (f32[2,2,64,512]{3,2,1,0:T(8,128)S(1)}, f32[2,2,64,512]{3,2,1,0:T(8,128)S(1)}, u32[]{:S(2)}, u32[]{:S(2)}) collective-permute-start(f32[2,2,64,512]{3,2,1,0:T(8,128)S(1)} %get-tuple-element.546), channel_id=1, source_target_pairs={{8,0},{16,8},{24,16},{9,1},{17,9},{25,17},{10,2},{18,10},{26,18},{... | collective-permute-start | bytes 1572872 | tf_op jit(solution)/shard_map/ppermute | solution.py:19
  29.6 0.6 copy-start.8
  29.8 0.6 copy-start.10
  29.9 0.6 copy-start.12
  37.1 6.3 %copy-start.9 = (bf16[128,128]{1,0:T(8,128)(2,1)S(1)}, bf16[128,128]{1,0:T(8,128)(2,1)}, u32[]{:S(2)}) copy-start(bf16[128,128]{1,0:T(8,128)(2,1)} %copy-done.8) | copy-start | bytes 98308
  37.2 6.3 %copy-start.11 = (bf16[128,128]{1,0:T(8,128)(2,1)S(1)}, bf16[128,128]{1,0:T(8,128)(2,1)}, u32[]{:S(2)}) copy-start(bf16[128,128]{1,0:T(8,128)(2,1)} %copy-done.10) | copy-start | bytes 98308
  37.2 6.3 %copy-start.13 = (bf16[128,128]{1,0:T(8,128)(2,1)S(1)}, bf16[128,128]{1,0:T(8,128)(2,1)}, u32[]{:S(2)}) copy-start(bf16[128,128]{1,0:T(8,128)(2,1)} %copy-done.12) | copy-start | bytes 98308
  37.2 6.3 %copy-start.14 = (pred[4,2]{0,1:T(4,128)(4,1)S(1)}, pred[4,2]{0,1:T(4,128)(4,1)}, u32[]{:S(2)}) copy-start(pred[4,2]{0,1:T(4,128)(4,1)} %reduce_or.9) | copy-start | bytes 28
  37.2 6.3 %copy-start.5 = (f32[4,2,128,128]{3,2,1,0:T(8,128)S(1)}, f32[4,2,128,128]{3,2,1,0:T(8,128)}, u32[]{:S(2)}) copy-start(f32[4,2,128,128]{3,2,1,0:T(8,128)} %param.8) | copy-start | bytes 1572868
  40.0 6.6 %collective-permute-start.2 = (f32[2,2,640,64]{2,3,1,0:T(8,128)}, f32[2,2,640,64]{2,3,1,0:T(8,128)}, u32[]{:S(2)}, u32[]{:S(2)}) collective-permute-start(f32[2,2,640,64]{2,3,1,0:T(8,128)} %get-tuple-element.543), channel_id=1, source_target_pairs={{0,1},{1,2},{2,3},{3,4},{4,5},{5,6},{6,7},{8,9},{9,10},{10,11},{11... | collective-permute-start | bytes 1966088 | tf_op jit(solution)/shard_map/ppermute | solution.py:16
  42.1 5.2 %collective-permute-start.3 = (f32[2,2,640,64]{2,3,1,0:T(8,128)}, f32[2,2,640,64]{2,3,1,0:T(8,128)}, u32[]{:S(2)}, u32[]{:S(2)}) collective-permute-start(f32[2,2,640,64]{2,3,1,0:T(8,128)} %get-tuple-element.544), channel_id=1, source_target_pairs={{1,0},{2,1},{3,2},{4,3},{5,4},{6,5},{7,6},{9,8},{10,9},{11,10},{12... | collective-permute-start | bytes 1966088 | tf_op jit(solution)/shard_map/ppermute | solution.py:19
  53.3 3.2 copy-start.15
  75.3 2.3 copy-start.4
  102.5 2.3 copy-start.4
  129.5 2.3 copy-start.4
  156.7 2.3 copy-start.4
  183.9 2.3 copy-start.4
  211.1 2.3 copy-start.4
  238.2 2.3 copy-start.4
  265.5 2.3 copy-start.4
  283.1 9.9 %collective-permute-start.4 = (f32[2,2,64,640]{3,2,1,0:T(8,128)S(1)}, f32[2,2,64,640]{3,2,1,0:T(8,128)S(1)}, u32[]{:S(2)}, u32[]{:S(2)}) collective-permute-start(f32[2,2,64,640]{3,2,1,0:T(8,128)S(1)} %slice.455), channel_id=1, source_target_pairs={{0,8},{8,16},{16,24},{1,9},{9,17},{17,25},{2,10},{10,18},{18,26},{... | collective-permute-start | bytes 1966088 | tf_op jit(solution)/shard_map/ppermute | solution.py:16
  295.3 13.1 %collective-permute-start.5 = (f32[2,2,64,640]{3,2,1,0:T(8,128)}, f32[2,2,64,640]{3,2,1,0:T(8,128)S(1)}, u32[]{:S(2)}, u32[]{:S(2)}) collective-permute-start(f32[2,2,64,640]{3,2,1,0:T(8,128)} %get-tuple-element.542), channel_id=1, source_target_pairs={{8,0},{16,8},{24,16},{9,1},{17,9},{25,17},{10,2},{18,10},{26,18},{... | collective-permute-start | bytes 1966088 | tf_op jit(solution)/shard_map/ppermute | solution.py:19
  314.0 15.1 %collective-permute-start.6 = (f32[2,2,512,64]{2,3,1,0:T(8,128)}, f32[2,2,512,64]{2,3,1,0:T(8,128)}, u32[]{:S(2)}, u32[]{:S(2)}) collective-permute-start(f32[2,2,512,64]{2,3,1,0:T(8,128)} %pad_maximum_fusion.6), channel_id=1, source_target_pairs={{0,1},{1,2},{2,3},{3,4},{4,5},{5,6},{6,7},{8,9},{9,10},{10,11},{11... | collective-permute-start | bytes 1572872 | tf_op jit(solution)/shard_map/ppermute | solution.py:16
  328.9 143.3 %copy-start.6 = (f32[4,2,128,128]{3,2,1,0:T(8,128)S(1)}, f32[4,2,128,128]{3,2,1,0:T(8,128)}, u32[]{:S(2)}) copy-start(f32[4,2,128,128]{3,2,1,0:T(8,128)} %param.8) | copy-start | bytes 1572868
  331.7 147.9 %collective-permute-start.7 = (f32[2,2,512,64]{2,3,1,0:T(8,128)}, f32[2,2,512,64]{2,3,1,0:T(8,128)}, u32[]{:S(2)}, u32[]{:S(2)}) collective-permute-start(f32[2,2,512,64]{2,3,1,0:T(8,128)} %get-tuple-element.540), channel_id=1, source_target_pairs={{1,0},{2,1},{3,2},{4,3},{5,4},{6,5},{7,6},{9,8},{10,9},{11,10},{12... | collective-permute-start | bytes 1572872 | tf_op jit(solution)/shard_map/ppermute | solution.py:19
  479.3 2.1 copy-start.2
  479.6 3.5 copy-start.3
  479.6 3.5 copy-start.7
  483.1 8.2 %copy-start.1 = (bf16[8,128,128]{2,1,0:T(8,128)(2,1)S(1)}, bf16[8,128,128]{2,1,0:T(8,128)(2,1)}, u32[]{:S(2)}) copy-start(bf16[8,128,128]{2,1,0:T(8,128)(2,1)} %param.9) | copy-start | bytes 786436
Sparse Core Ops, SparseCore 0:
  329.0 140.7 all-reduce.1
where the time goes:
time: 503 us; the launch traced here: 498 us
  waiting for transfers between devices  159 us (32%)
  local copies, waits for them, and re-layouts  119 us (24%)
  other arithmetic  88.5 us (18%)
  matrix products  49.7 us (10%)
  starting transfers between devices  33.7 us (7%)
  loops' own time  32.6 us (6%)
  between operations  15.8 us (3%)
    psum x1, waiting for transfers between devices, on_device(): summed = lax.psum(probe_grad, ('ty', 'tx'))  137 us
    dot_general x48, matrix products, transform(): jnp.einsum('ij,bjq->biq', left_table, partial_value, preferred_element_ty...  49.5 us
    dynamic_update_slice x8, local copies, waits for them, and re-layouts, visit_slot(): gradient = lax.dynamic_update_slice(gradient, current + slice_grads, corner)  34.9 us
    another operation x1, loops' own time, on_device(): lax.scan(visit_slot, initial, (incoming, local_row, local_col, slot_live....  32.6 us
    dynamic_slice x40, local copies, waits for them, and re-layouts, on_device(): lax.scan(visit_slot, initial, (incoming, local_row, local_col, slot_live....  26.4 us
    ppermute x4, starting transfers between devices, extended_2(): lax.ppermute(lax.slice_in_dim(block, block.shape[dim] - width, None, axis...  22 us
    squeeze x48, other arithmetic, transform(): joined = jnp.concatenate([rounded[:, 0], rounded[:, 1]], axis=-1)  20.9 us
    unnamed x33, local copies, waits for them, and re-layouts  12.9 us
  transfers between devices with their start and end apart: 10, of which 7 were waited for; matrix products, arithmetic and copies ran while one was open for 7% of the time, Pallas kernels for 0%

commit v1 on v0

--- a/solution.py
+++ b/solution.py
@@ -207,7 +207,7 @@
     )
     probe_power = jnp.mean(jnp.sum(probe_modes**2, axis=(0, 1)))
     new_object = object_slices - folded / (probe_power + 1e-06)
-    summed = lax.psum(probe_grad, ("ty", "tx"))
+    summed = lax.psum(lax.psum(probe_grad, "tx"), "ty")
     spread = jnp.sqrt(jnp.mean(summed * summed) + 1e-06)
     new_probe = probe_modes - 0.5 * summed / spread
     return (new_object, new_probe)

time: 503 us -> 469 us (0.932)
  waiting for transfers between devices: 159 us -> 125 us
    psum x1 -> x2, waiting for transfers between devices: 137 us -> 103 us  [on_device(): summed = lax.psum(lax.psum(probe_grad, 'tx'), 'ty')]
  transfers between devices with their start and end apart: 10 -> 11, of which waited for: 7 -> 7; matrix products, arithmetic and copies ran while one was open for 7% -> 8% of each run, Pallas kernels for 0% -> 0%
where the time goes in v1:
time: 469 us; the launch traced here: 464 us
  waiting for transfers between devices  125 us (27%)
  local copies, waits for them, and re-layouts  119 us (25%)
  other arithmetic  88.6 us (19%)
  matrix products  49.7 us (11%)
  starting transfers between devices  33.7 us (7%)
  loops' own time  32.6 us (7%)
  between operations  15.8 us (3%)
    psum x2, waiting for transfers between devices, on_device(): summed = lax.psum(lax.psum(probe_grad, 'tx'), 'ty')  103 us
    dot_general x48, matrix products, transform(): jnp.einsum('ij,bjq->biq', left_table, partial_value, preferred_element_ty...  49.5 us
    dynamic_update_slice x8, local copies, waits for them, and re-layouts, visit_slot(): gradient = lax.dynamic_update_slice(gradient, current + slice_grads, corner)  34.9 us
    another operation x1, loops' own time, on_device(): lax.scan(visit_slot, initial, (incoming, local_row, local_col, slot_live....  32.6 us
    dynamic_slice x40, local copies, waits for them, and re-layouts, on_device(): lax.scan(visit_slot, initial, (incoming, local_row, local_col, slot_live....  26.4 us
    ppermute x4, starting transfers between devices, extended_2(): lax.ppermute(lax.slice_in_dim(block, block.shape[dim] - width, None, axis...  22 us
    squeeze x48, other arithmetic, transform(): joined = jnp.concatenate([rounded[:, 0], rounded[:, 1]], axis=-1)  20.9 us
    unnamed x33, local copies, waits for them, and re-layouts  12.9 us
  transfers between devices with their start and end apart: 11, of which 7 were waited for; matrix products, arithmetic and copies ran while one was open for 8% of the time, Pallas kernels for 0%

profile of v1, /device:TPU:0, one launch (start us, length us, event | category | flops | bytes accessed | tf_op | source)
XLA Modules:
  0.0 464.2 jit_solution(6345001081023153027)
XLA Ops:
  10.3 6.3 %all-to-all-start = ((bf16[8,128,128]{2,1,0:T(8,128)(2,1)}), bf16[8,128,128]{2,1,0:T(8,128)(2,1)}, u32[]{:S(2)}, u32[]{:S(2)}) async-start(bf16[8,128,128]{2,1,0:T(8,128)(2,1)} %copy.108), calls=%async_computation | async-start | bytes 524288 | tf_op jit(solution)/shard_map/all_to_all | solution.py:154
  18.0 4.0 collective-permute-start
  23.2 5.2 %copy.120 = f32[2,2,512,512]{2,3,1,0:T(8,128)} copy(f32[2,2,512,512]{3,2,1,0:T(8,128)} %param.7) | data formatting | bytes 8388608 | tf_op args[0]
  30.5 2.0 collective-permute-done
  32.8 4.0 collective-permute-done.1
  37.2 2.8 pad_maximum_fusion.4
  40.0 2.1 collective-permute-start.2
  47.4 5.9 %pad_maximum_fusion = f32[2,2,640,640]{2,3,1,0:T(8,128)} fusion(f32[2,2,640,64]{2,3,1,0:T(8,128)} %collective-permute-done.3, f32[2,2,64,512]{2,3,1,0:T(8,128)S(1)} %copy.106, f32[2,2,512,512]{2,3,1,0:T(8,128)} %copy.120, f32[2,2,64,512]{2,3,1,0:T(8,128)S(1)} %copy.104, f32[2,2,640,64]{2,3,1,0:T(8,128)} %collective-permute-done.2), kind=kLoop, calls=%fused_computation.110 | loop fusion | flops 6553600 | bytes 13107200 | tf_op jit(solution)/shard_map/concatenate | solution.py:20
  53.3 3.2 broadcast_in_dim.8
  56.5 217.4 %while.18 = (s32[]{:T(128)}, f32[2,2,640,640]{2,3,1,0:T(8,128)}, f32[4,2,128,128]{3,2,0,1:T(8,128)S(1)}, s32[8]{0:T(128)S(1)}, s32[8]{0:T(128)S(1)}, /*index=5*/...) while((s32[]{:T(128)}, f32[2,2,640,640]{2,3,1,0:T(8,128)}, ...), condition=%wide.region_8.9_spmd.clone.clone.clone.clone, body=%wide.region_4.8_spmd.clone.clone.clone.clone.sunk | while | flops 815677440 | bytes 33391468 | solution.py:187
  67.7 1.5 convolution_bitcast_fusion.13
  70.0 1.5 convolution_bitcast_fusion.14
  73.7 1.5 convolution_bitcast_fusion.15
  79.3 4.4 dynamic_update_slice.10
  94.9 1.5 convolution_bitcast_fusion.13
  97.1 1.5 convolution_bitcast_fusion.14
  100.9 1.5 convolution_bitcast_fusion.15
  106.5 4.2 dynamic_update_slice.10
  121.9 1.5 convolution_bitcast_fusion.13
  124.2 1.5 convolution_bitcast_fusion.14
  127.9 1.5 convolution_bitcast_fusion.15
  133.5 4.4 dynamic_update_slice.10
  149.1 1.5 convolution_bitcast_fusion.13
  151.4 1.5 convolution_bitcast_fusion.14
  152.9 1.5 fusion.155
  155.1 1.5 convolution_bitcast_fusion.15
  160.7 4.4 dynamic_update_slice.10
  176.3 1.5 convolution_bitcast_fusion.13
  178.6 1.5 convolution_bitcast_fusion.14
  182.3 1.5 convolution_bitcast_fusion.15
  187.9 4.4 dynamic_update_slice.10
  203.5 1.5 convolution_bitcast_fusion.13
  205.7 1.5 convolution_bitcast_fusion.14
  209.5 1.5 convolution_bitcast_fusion.15
  215.1 4.3 dynamic_update_slice.10
  230.6 1.5 convolution_bitcast_fusion.13
  232.9 1.5 convolution_bitcast_fusion.14
  236.6 1.5 convolution_bitcast_fusion.15
  242.2 4.4 dynamic_update_slice.10
  257.8 1.5 convolution_bitcast_fusion.13
  260.1 1.5 convolution_bitcast_fusion.14
  263.9 1.5 convolution_bitcast_fusion.15
  269.4 4.4 dynamic_update_slice.10
  273.8 8.2 %copy.114 = f32[2,2,640,640]{3,2,1,0:T(8,128)} copy(f32[2,2,640,640]{2,3,1,0:T(8,128)} %get-tuple-element.206) | data formatting | bytes 13107200 | tf_op jit(solution)/shard_map/while | solution.py:187
  283.1 1.9 collective-permute-start.4
  285.0 8.0 %collective-permute-done.4 = f32[2,2,64,640]{3,2,1,0:T(8,128)S(1)} collective-permute-done((f32[2,2,64,640]{3,2,1,0:T(8,128)S(1)}, f32[2,2,64,640]{3,2,1,0:T(8,128)S(1)}, u32[]{:S(2)}, u32[]{:S(2)}) %collective-permute-start.4) | collective-permute-done | bytes 655392 | tf_op jit(solution)/shard_map/ppermute | solution.py:16
  293.1 2.3 slice_add_fusion.7
  295.3 1.5 collective-permute-start.5
  296.8 4.2 slice.281
  301.4 7.1 %collective-permute-done.5 = f32[2,2,64,640]{3,2,1,0:T(8,128)S(1)} collective-permute-done((f32[2,2,64,640]{3,2,1,0:T(8,128)}, f32[2,2,64,640]{3,2,1,0:T(8,128)S(1)}, u32[]{:S(2)}, u32[]{:S(2)}) %collective-permute-start.5) | collective-permute-done | bytes 655392 | tf_op jit(solution)/shard_map/ppermute | solution.py:19
  308.5 2.0 slice_add_fusion.6
  310.5 1.5 copy.119
  312.0 2.0 pad_maximum_fusion.6
  314.0 14.0 %collective-permute-start.6 = (f32[2,2,512,64]{2,3,1,0:T(8,128)}, f32[2,2,512,64]{2,3,1,0:T(8,128)}, u32[]{:S(2)}, u32[]{:S(2)}) collective-permute-start(f32[2,2,512,64]{2,3,1,0:T(8,128)} %pad_maximum_fusion.6), channel_id=1, source_target_pairs={{0,1},{1,2},{2,3},{3,4},{4,5},{5,6},{6,7},{8,9},{9,10},{10,11},{11... | collective-permute-start | bytes 1572872 | tf_op jit(solution)/shard_map/ppermute | solution.py:16
  328.9 66.6 %all-reduce.3.cloned.1.call-done = f32[4,2,128,128]{3,2,1,0:T(8,128)} async-done(((f32[4,2,128,128]{3,2,1,0:T(8,128)}), f32[4,2,128,128]{3,2,1,0:T(8,128)}) %all-reduce.3.cloned.1.call-update) | async-done | bytes 524304 | tf_op jit(solution)/shard_map/psum | solution.py:210
  395.6 2.7 maximum_add_fusion.3
  399.6 36.1 %all-reduce.5.cloned.1.call-done = f32[4,2,128,128]{3,2,1,0:T(8,128)} async-done(((f32[4,2,128,128]{3,2,1,0:T(8,128)}), f32[4,2,128,128]{3,2,1,0:T(8,128)}) %all-reduce.5.cloned.1.call-update) | async-done | bytes 524304 | tf_op jit(solution)/shard_map/psum | solution.py:210
  435.7 1.8 multiply_reduce_fusion
  438.2 2.6 divide_subtract_fusion
  441.4 3.9 pad_maximum_fusion.1
  445.7 1.8 copy-done.2
  447.4 1.7 maximum_add_fusion.2
  449.2 3.0 fusion.85
  452.1 5.2 %copy.122 = f32[2,2,512,512]{3,2,1,0:T(8,128)} copy(f32[2,2,512,512]{2,3,1,0:T(8,128)} %fusion.85) | data formatting | bytes 8388608
  (358 shorter events, 130.0 us)
Async XLA Ops:
  7.2 2.1 copy-start
  10.3 43.0 %all-to-all-start = ((bf16[8,128,128]{2,1,0:T(8,128)(2,1)}), bf16[8,128,128]{2,1,0:T(8,128)(2,1)}, u32[]{:S(2)}, u32[]{:S(2)}) async-start(bf16[8,128,128]{2,1,0:T(8,128)(2,1)} %copy.108), calls=%async_computation | async-start | bytes 524288 | tf_op jit(solution)/shard_map/all_to_all | solution.py:154
  16.7 378.8 %all-reduce.3.cloned.1.call-start = ((), (), s32[]{:S(2)}) async-start(), calls=%async_computation.1 | async-start | bytes 1048576 | tf_op jit(solution)/shard_map/psum | solution.py:210
  18.0 14.5 %collective-permute-start = (f32[2,2,64,512]{3,2,1,0:T(8,128)S(1)}, f32[2,2,64,512]{3,2,1,0:T(8,128)S(1)}, u32[]{:S(2)}, u32[]{:S(2)}) collective-permute-start(f32[2,2,64,512]{3,2,1,0:T(8,128)S(1)} %get-tuple-element.545), channel_id=1, source_target_pairs={{0,8},{8,16},{16,24},{1,9},{9,17},{17,25},{2,10},{10,18},{18,26},{... | collective-permute-start | bytes 1572872 | tf_op jit(solution)/shard_map/ppermute | solution.py:16
  21.9 14.9 %collective-permute-start.1 = (f32[2,2,64,512]{3,2,1,0:T(8,128)S(1)}, f32[2,2,64,512]{3,2,1,0:T(8,128)S(1)}, u32[]{:S(2)}, u32[]{:S(2)}) collective-permute-start(f32[2,2,64,512]{3,2,1,0:T(8,128)S(1)} %get-tuple-element.546), channel_id=1, source_target_pairs={{8,0},{16,8},{24,16},{9,1},{17,9},{25,17},{10,2},{18,10},{26,18},{... | collective-permute-start | bytes 1572872 | tf_op jit(solution)/shard_map/ppermute | solution.py:19
  29.6 0.6 copy-start.8
  29.8 0.6 copy-start.10
  29.9 0.6 copy-start.12
  37.1 6.3 %copy-start.9 = (bf16[128,128]{1,0:T(8,128)(2,1)S(1)}, bf16[128,128]{1,0:T(8,128)(2,1)}, u32[]{:S(2)}) copy-start(bf16[128,128]{1,0:T(8,128)(2,1)} %copy-done.8) | copy-start | bytes 98308
  37.2 6.3 %copy-start.11 = (bf16[128,128]{1,0:T(8,128)(2,1)S(1)}, bf16[128,128]{1,0:T(8,128)(2,1)}, u32[]{:S(2)}) copy-start(bf16[128,128]{1,0:T(8,128)(2,1)} %copy-done.10) | copy-start | bytes 98308
  37.2 6.3 %copy-start.13 = (bf16[128,128]{1,0:T(8,128)(2,1)S(1)}, bf16[128,128]{1,0:T(8,128)(2,1)}, u32[]{:S(2)}) copy-start(bf16[128,128]{1,0:T(8,128)(2,1)} %copy-done.12) | copy-start | bytes 98308
  37.2 6.3 %copy-start.14 = (pred[4,2]{0,1:T(4,128)(4,1)S(1)}, pred[4,2]{0,1:T(4,128)(4,1)}, u32[]{:S(2)}) copy-start(pred[4,2]{0,1:T(4,128)(4,1)} %reduce_or.9) | copy-start | bytes 28
  37.2 6.3 %copy-start.5 = (f32[4,2,128,128]{3,2,1,0:T(8,128)S(1)}, f32[4,2,128,128]{3,2,1,0:T(8,128)}, u32[]{:S(2)}) copy-start(f32[4,2,128,128]{3,2,1,0:T(8,128)} %param.8) | copy-start | bytes 1572868
  40.0 6.6 %collective-permute-start.2 = (f32[2,2,640,64]{2,3,1,0:T(8,128)}, f32[2,2,640,64]{2,3,1,0:T(8,128)}, u32[]{:S(2)}, u32[]{:S(2)}) collective-permute-start(f32[2,2,640,64]{2,3,1,0:T(8,128)} %get-tuple-element.543), channel_id=1, source_target_pairs={{0,1},{1,2},{2,3},{3,4},{4,5},{5,6},{6,7},{8,9},{9,10},{10,11},{11... | collective-permute-start | bytes 1966088 | tf_op jit(solution)/shard_map/ppermute | solution.py:16
  42.1 5.2 %collective-permute-start.3 = (f32[2,2,640,64]{2,3,1,0:T(8,128)}, f32[2,2,640,64]{2,3,1,0:T(8,128)}, u32[]{:S(2)}, u32[]{:S(2)}) collective-permute-start(f32[2,2,640,64]{2,3,1,0:T(8,128)} %get-tuple-element.544), channel_id=1, source_target_pairs={{1,0},{2,1},{3,2},{4,3},{5,4},{6,5},{7,6},{9,8},{10,9},{11,10},{12... | collective-permute-start | bytes 1966088 | tf_op jit(solution)/shard_map/ppermute | solution.py:19
  53.3 3.2 copy-start.15
  75.3 2.3 copy-start.4
  102.5 2.3 copy-start.4
  129.5 2.3 copy-start.4
  156.7 2.3 copy-start.4
  183.9 2.3 copy-start.4
  211.1 2.3 copy-start.4
  238.2 2.3 copy-start.4
  265.5 2.3 copy-start.4
  283.1 9.9 %collective-permute-start.4 = (f32[2,2,64,640]{3,2,1,0:T(8,128)S(1)}, f32[2,2,64,640]{3,2,1,0:T(8,128)S(1)}, u32[]{:S(2)}, u32[]{:S(2)}) collective-permute-start(f32[2,2,64,640]{3,2,1,0:T(8,128)S(1)} %slice.455), channel_id=1, source_target_pairs={{0,8},{8,16},{16,24},{1,9},{9,17},{17,25},{2,10},{10,18},{18,26},{... | collective-permute-start | bytes 1966088 | tf_op jit(solution)/shard_map/ppermute | solution.py:16
  295.3 13.1 %collective-permute-start.5 = (f32[2,2,64,640]{3,2,1,0:T(8,128)}, f32[2,2,64,640]{3,2,1,0:T(8,128)S(1)}, u32[]{:S(2)}, u32[]{:S(2)}) collective-permute-start(f32[2,2,64,640]{3,2,1,0:T(8,128)} %get-tuple-element.542), channel_id=1, source_target_pairs={{8,0},{16,8},{24,16},{9,1},{17,9},{25,17},{10,2},{18,10},{26,18},{... | collective-permute-start | bytes 1966088 | tf_op jit(solution)/shard_map/ppermute | solution.py:19
  314.0 81.6 %collective-permute-start.6 = (f32[2,2,512,64]{2,3,1,0:T(8,128)}, f32[2,2,512,64]{2,3,1,0:T(8,128)}, u32[]{:S(2)}, u32[]{:S(2)}) collective-permute-start(f32[2,2,512,64]{2,3,1,0:T(8,128)} %pad_maximum_fusion.6), channel_id=1, source_target_pairs={{0,1},{1,2},{2,3},{3,4},{4,5},{5,6},{6,7},{8,9},{9,10},{10,11},{11... | collective-permute-start | bytes 1572872 | tf_op jit(solution)/shard_map/ppermute | solution.py:16
  328.9 106.8 %all-reduce.5.cloned.1.call-start = ((), (), s32[]{:S(2)}) async-start(), calls=%async_computation.2 | async-start | bytes 1048576 | tf_op jit(solution)/shard_map/psum | solution.py:210
  395.5 42.7 %copy-start.6 = (f32[4,2,128,128]{3,2,1,0:T(8,128)S(1)}, f32[4,2,128,128]{3,2,1,0:T(8,128)}, u32[]{:S(2)}) copy-start(f32[4,2,128,128]{3,2,1,0:T(8,128)} %param.8) | copy-start | bytes 1572868
  398.3 47.4 %collective-permute-start.7 = (f32[2,2,512,64]{2,3,1,0:T(8,128)}, f32[2,2,512,64]{2,3,1,0:T(8,128)}, u32[]{:S(2)}, u32[]{:S(2)}) collective-permute-start(f32[2,2,512,64]{2,3,1,0:T(8,128)} %get-tuple-element.540), channel_id=1, source_target_pairs={{1,0},{2,1},{3,2},{4,3},{5,4},{6,5},{7,6},{9,8},{10,9},{11,10},{12... | collective-permute-start | bytes 1572872 | tf_op jit(solution)/shard_map/ppermute | solution.py:19
  445.3 2.1 copy-start.2
  445.6 3.5 copy-start.3
  445.7 3.5 copy-start.7
  449.1 8.2 %copy-start.1 = (bf16[8,128,128]{2,1,0:T(8,128)(2,1)S(1)}, bf16[8,128,128]{2,1,0:T(8,128)(2,1)}, u32[]{:S(2)}) copy-start(bf16[8,128,128]{2,1,0:T(8,128)(2,1)} %param.9) | copy-start | bytes 786436
Sparse Core Ops, SparseCore 0:
  329.0 66.4 all-reduce.2
  397.9 37.8 all-reduce.4
